TPU v7x, 32 devices: a whole 2x2x4 slice. The times are simulated.
32 devices in a mesh: frame: 4 (over z), space: 8 (over y, x, core).
Axes of the slice: x: 2, y: 2, z: 4, core: 2. Of those that a mesh axis runs over, the one named last changes fastest.
Arguments:
- tokens: bfloat16 [32, 152, 1024], P('space', 'frame'), may hold values from -16 to 16
- tube_count: int32 [8], P('space'), may hold values from 1 to 4, as said below
- ln_gain: float32 [1024], replicated, may hold values from 0.25 to 1.75
- ln_bias: float32 [1024], replicated, may hold values from -3 to 3
- w_qkv: bfloat16 [1024, 1536], replicated, may hold values from -1.5 to 1.5
- w_out: bfloat16 [512, 1024], replicated, may hold values from -0.25 to 0.25
Outputs:
- mixed: bfloat16 [32, 152, 1024], P('space', 'frame')
Inputs may be any that keep to these rules, and one draw needn't show every extreme that they name: tube_count[s] is how many of the 4 slots of space index s hold visible tubes; they are the first ones. Some index has all 4, some only 1.
All inputs are finite; a program needn't handle non-finite values.
Results may differ from a plain program's by a relative error of at most 0.005.
Values may be sent and summed in bfloat16 or wider, within the bound.
No kernel may reach another device: no remote copies, remote signals or barrier semaphores. Data moves between devices by JAX's collectives and lax.ppermute only.
A program may use at most 128 MiB of HBM per device.

v0:
```python
import jax
import jax.numpy as jnp
from jax import lax
from jax.sharding import PartitionSpec as P

HEADS = 8
EPSILON = 1e-06
NEG_FILL = -1e30


def layer_norm(flat, ln_gain, ln_bias):
    values32 = flat.astype(jnp.float32)
    center = values32 - jnp.mean(values32, axis=-1, keepdims=True)
    spread = jnp.mean(center * center, axis=-1, keepdims=True)
    return (center * lax.rsqrt(spread + EPSILON) * ln_gain + ln_bias).astype(jnp.bfloat16)


def live_mask(counts, slots_dev, time_dev):
    slot_ids = jnp.arange(slots_dev)[None, :, None]
    marks = jnp.broadcast_to(
        slot_ids < counts[:, None, None], (counts.shape[0], slots_dev, time_dev)
    )
    return marks.reshape(-1)


def attend(carry, query_heads, key_block, value_block, live_keys, scaling):
    best_now, total_now, accum = carry
    heads = query_heads.shape[1]
    key_heads = key_block.reshape(key_block.shape[0], heads, -1)
    value_heads = value_block.reshape(value_block.shape[0], heads, -1)
    scores = (
        jnp.einsum("qhd,khd->hqk", query_heads, key_heads, preferred_element_type=jnp.float32)
        * scaling
    )
    scores = jnp.where(live_keys[None, None, :], scores, NEG_FILL)
    best_next = jnp.maximum(best_now, jnp.max(scores, axis=-1))
    fading = jnp.exp(best_now - best_next)
    weights = jnp.exp(scores - best_next[..., None])
    total_next = total_now * fading + jnp.sum(weights, axis=-1)
    accum = accum * fading[..., None] + jnp.einsum(
        "hqk,khd->hqd",
        weights.astype(jnp.bfloat16),
        value_heads,
        preferred_element_type=jnp.float32,
    )
    return (best_next, total_next, accum)


def make_fold(query_heads, vis_dev, time_dev, scaling):
    rows_dev = vis_dev * time_dev

    def fold_masked(carry, piece, start):
        key_all, value_all, count_all = piece
        width_in = key_all.shape[1]
        shards = count_all.shape[0]
        group = 1
        for unused_bit in range(6):
            if shards % (group * 2) == 0 and group * rows_dev < 2048:
                group = group * 2
        blocks = shards // group
        key_groups = key_all.reshape(blocks, group * rows_dev, width_in)
        value_groups = value_all.reshape(blocks, group * rows_dev, width_in)
        count_groups = count_all.reshape(blocks, group)

        def step_group(state, item):
            key_group, value_group, count_group = item
            marks = live_mask(count_group, vis_dev, time_dev)
            return (attend(state, query_heads, key_group, value_group, marks, scaling), None)

        carry, unused = lax.scan(step_group, carry, (key_groups, value_groups, count_groups))
        return carry

    return fold_masked


def start_state(heads, rows, head_size):
    return (
        jnp.full((heads, rows), NEG_FILL, jnp.float32),
        jnp.zeros((heads, rows), jnp.float32),
        jnp.zeros((heads, rows, head_size), jnp.float32),
    )


def on_device(tokens, tube_count, ln_gain, ln_bias, w_qkv, w_out):
    vis_dev, time_dev, width = tokens.shape
    rows_dev = vis_dev * time_dev
    inner = w_out.shape[0]
    head_size = inner // HEADS
    flat = tokens.reshape(rows_dev, width)
    normed = layer_norm(flat, ln_gain, ln_bias)
    projected = jnp.dot(normed, w_qkv, preferred_element_type=jnp.float32).astype(jnp.bfloat16)
    scaling = head_size ** (-0.5)
    frames = lax.axis_size("frame")
    local_heads = HEADS // frames
    stacked = projected.reshape(rows_dev, 3, HEADS, head_size)
    regrouped = lax.all_to_all(stacked, "frame", split_axis=2, concat_axis=0, tiled=True)
    all_rows = regrouped.shape[0]
    query_local = regrouped[:, 0]
    key_local = regrouped[:, 1].reshape(all_rows, local_heads * head_size)
    value_local = regrouped[:, 2].reshape(all_rows, local_heads * head_size)
    counts_rep = jnp.tile(tube_count, frames)
    fold_fn = make_fold(query_local, vis_dev, time_dev, scaling)
    state = fold_fn(
        start_state(local_heads, all_rows, head_size),
        (
            lax.all_gather(key_local, "space", axis=0, tiled=True),
            lax.all_gather(value_local, "space", axis=0, tiled=True),
            lax.all_gather(counts_rep, "space", axis=0, tiled=True),
        ),
        jnp.int32(0),
    )
    best_final, total_final, accum_final = state
    attended = (accum_final / total_final[..., None]).astype(jnp.bfloat16)
    attended = jnp.transpose(attended, (1, 0, 2))
    returned = lax.all_to_all(attended, "frame", split_axis=0, concat_axis=1, tiled=True)
    attended = returned.reshape(rows_dev, inner)
    mixed = flat.astype(jnp.float32) + jnp.dot(attended, w_out, preferred_element_type=jnp.float32)
    own_live = live_mask(tube_count, vis_dev, time_dev)
    mixed = jnp.where(own_live[:, None], mixed, 0.0)
    return mixed.astype(jnp.bfloat16).reshape(vis_dev, time_dev, width)


def solution(mesh):
    in_specs = (P("space", "frame", None), P("space"), P(), P(), P(), P())
    out_specs = P("space", "frame", None)
    return jax.shard_map(
        on_device, mesh=mesh, in_specs=in_specs, out_specs=out_specs, check_vma=False
    )
```

profile of v0, /device:TPU:0, one launch (start us, length us, event | category | flops | bytes accessed | tf_op | source)
XLA Modules:
  0.0 166.7 jit_solution(1666170860876456033)
XLA Ops:
  6.5 1.3 convert_reduce_fusion
  7.9 0.1 copy.60
  8.0 1.3 multiply_reduce_fusion
  9.3 1.9 %copy.42 = f32[4,38,1024]{2,1,0:T(8,128)} copy(bf16[4,38,1024]{2,0,1:T(4,128)(2,1)} %param.8) | data formatting | bytes 933888 | tf_op jit(solution)/shard_map/convert_element_type | solution.py:117
  11.3 0.1 copy.61
  11.4 2.0 %reshape.120 = f32[152,1024]{1,0:T(8,128)} reshape(f32[4,38,1024]{2,1,0:T(8,128)} %copy.42) | data formatting | bytes 1245184 | tf_op jit(solution)/shard_map/convert_element_type | solution.py:117
  13.4 2.6 %convolution_convert_fusion = bf16[152,1536]{1,0:T(8,128)(2,1)} fusion(bf16[1024,1536]{1,0:T(8,128)(2,1)S(1)} %copy-done, f32[152,1024]{1,0:T(8,128)} %reshape.120, f32[1024]{0:T(1024)} %param.11, f32[1024]{0:T(1024)} %param.10, f32[152]{0:T(256)S(1)} %rsqrt.12, f32[152]{0:T(256)S(1)} %div.17), kind=kOutput, calls=%fused_computation.22 | convolution fusion | flops 479162368 | bytes 4244672 | tf_op jit(solution)/shard_map/dot_general | solution.py:91
  16.1 2.4 %reshape.115 = bf16[152,3,8,64]{3,2,1,0:T(8,128)(2,1)} reshape(bf16[152,1536]{1,0:T(8,128)(2,1)} %convolution_convert_fusion) | data formatting | bytes 933888 | tf_op jit(solution)/shard_map/reshape | solution.py:95
  18.4 2.8 %copy.46 = bf16[152,3,8,64]{0,3,1,2:T(8,128)(2,1)} copy(bf16[152,3,8,64]{3,2,1,0:T(8,128)(2,1)} %reshape.115) | data formatting | bytes 933888 | tf_op jit(solution)/shard_map/reshape | solution.py:95
  21.3 26.5 %all_to_all.33 = bf16[152,3,8,64]{0,3,1,2:T(8,128)(2,1)S(1)} all-to-all(bf16[152,3,8,64]{0,3,1,2:T(8,128)(2,1)} %copy.46), channel_id=1, replica_groups=mesh['frame'=4,'space'=8] {'frame'}, dimensions={2} | all-to-all | bytes 933888 | tf_op jit(solution)/shard_map/all_to_all | solution.py:96
  47.7 1.5 copy.47
  49.2 2.7 %all_to_all.27 = bf16[608,3,2,64]{0,3,2,1:T(8,128)(2,1)} reshape(bf16[4,152,3,2,64]{1,0,4,3,2:T(4,128)(2,1)} %copy.47) | data formatting | bytes 933888 | tf_op jit(solution)/shard_map/all_to_all | solution.py:96
  51.9 1.8 %fusion.20 = (bf16[608,1,2,64]{0,3,2,1:T(8,128)(2,1)}, bf16[608,2,64]{0,2,1:T(8,128)(2,1)S(1)}, bf16[608,1,2,64]{0,3,2,1:T(8,128)(2,1)S(1)}) fusion(bf16[608,3,2,64]{0,3,2,1:T(8,128)(2,1)} %all_to_all.27), kind=kLoop, calls=%fused_computation.40 | loop fusion | bytes 933888 | tf_op jit(solution)/shard_map/slice | solution.py:100
  53.7 1.7 %copy.49 = bf16[608,128]{1,0:T(8,128)(2,1)} copy(bf16[608,128]{0,1:T(8,128)(2,1)} %bitcast.69) | data formatting | bytes 311296 | tf_op jit(solution)/shard_map/reshape;squeeze | solution.py:100
  55.4 0.8 copy.48
  57.0 0.6 dynamic-slice
  58.3 8.1 %all-reduce = s32[32]{0:T(128)S(1)} all-reduce(s32[32]{0:T(128)S(1)} %broadcast_dynamic-update-slice_fusion), channel_id=1, replica_groups=mesh['frame'=4,'space'=8] {'space'}, use_global_device_ids=true, to_apply=%add | all-reduce | flops 32 | bytes 256
  66.5 12.4 %all-gather.5.cloned.1.call-done = bf16[4864,128]{1,0:T(8,128)(2,1)} async-done(((bf16[608,128]{1,0:T(8,128)(2,1)}), bf16[4864,128]{1,0:T(8,128)(2,1)}) %all-gather.5.cloned.1.call-update) | async-done | bytes 1245200 | tf_op jit(solution)/shard_map/all_gather | solution.py:107
  78.8 26.1 %all-gather.3.cloned.1.call-done = bf16[4864,128]{1,0:T(8,128)(2,1)} async-done(((bf16[608,128]{1,0:T(8,128)(2,1)}), bf16[4864,128]{1,0:T(8,128)(2,1)}) %all-gather.3.cloned.1.call-update) | async-done | bytes 1245200 | tf_op jit(solution)/shard_map/all_gather | solution.py:106
  105.0 32.1 %while.15 = (s32[]{:T(128)}, f32[2,608]{1,0:T(2,128)S(1)}, f32[2,608]{1,0:T(2,128)S(1)}, f32[2,608,64]{1,2,0:T(8,128)}, s32[2,16]{1,0:T(2,128)S(1)}, /*index=5*/...) while((s32[]{:T(128)}, f32[2,608]{1,0:T(2,128)S(1)}, ...), condition=%wide.region_5.6_spmd.clone, body=%wide.region_2.5_spmd.clone.sunk | while | flops 789841920 | bytes 47565588 | solution.py:70
  105.1 0.1 broadcast_in_dim.100
  105.3 2.4 %constant_dynamic-slice_fusion.4 = (bf16[1,2432,128]{2,1,0:T(8,128)(2,1)}, bf16[1,2432,128]{2,1,0:T(8,128)(2,1)}) fusion(bf16[2,2432,128]{2,1,0:T(8,128)(2,1)} %get-tuple-element.222, s32[]{:T(128)S(6)} %copy.73, bf16[2,2432,128]{2,1,0:T(8,128)(2,1)} %get-tuple-element.220), kind=kLoop, calls=%fused_computation.16.clone.1 | loop fusion | bytes 2490372 | tf_op jit(solution)/shard_map/while/body/jit(dynamic_index_in_dim)/dynamic_slice | solution.py:70
  107.7 2.1 %copy.66 = bf16[1,2432,128]{1,2,0:T(8,128)(2,1)} copy(bf16[1,2432,128]{2,1,0:T(8,128)(2,1)} %get-tuple-element.189) | data formatting | bytes 1245184 | tf_op jit(solution)/shard_map/while/body/jit(dynamic_index_in_dim)/dynamic_slice | solution.py:70
  109.8 2.1 %copy.67 = bf16[1,2432,128]{1,2,0:T(8,128)(2,1)} copy(bf16[1,2432,128]{2,1,0:T(8,128)(2,1)} %get-tuple-element.193) | data formatting | bytes 1245184 | tf_op jit(solution)/shard_map/while/body/jit(dynamic_index_in_dim)/dynamic_slice | solution.py:70
  111.9 3.1 %bitcast_reduce_fusion.2 = (f32[2,608]{1,0:T(2,128)S(1)}, f32[2,2432,608]{1,2,0:T(8,128)S(1)}) fusion(pred[2432]{0:T(1024)(128)(4,1)S(1)} %broadcast_in_dim.100, bf16[2432,2,64]{0,2,1:T(8,128)(2,1)} %bitcast.60, bf16[608,2,64]{0,2,1:T(8,128)(2,1)S(1)} %get-tuple-element.221), kind=kOutput, calls=%fused_computation.1.clone.1 | convolution fusion | flops 387406656 | bytes 12614784 | tf_op jit(solution)/shard_map/while/body/eval_jaxpr/qhd,khd->hqk/dot_general | solution.py:32
  115.1 2.5 %fusion.42 = f32[2,608]{1,0:T(2,128)S(1)} fusion(f32[2,2432,608]{1,2,0:T(8,128)S(1)} %get-tuple-element.191, f32[2,608]{1,0:T(2,128)S(1)} %fusion.41, pred[2432]{0:T(1024)(128)(4,1)S(1)} %broadcast_in_dim.100), kind=kLoop, calls=%fused_computation.5.clone.1 | loop fusion | flops 11828032 | bytes 11841408 | tf_op jit(solution)/shard_map/while/body/eval_jaxpr/reduce_sum | solution.py:39
  117.6 2.6 %fusion.44 = f32[2,608,64]{1,2,0:T(8,128)S(1)} fusion(bf16[2432,2,64]{0,2,1:T(8,128)(2,1)S(1)} %bitcast.61, f32[2,2432,608]{1,2,0:T(8,128)S(1)} %get-tuple-element.191, f32[2,608]{1,0:T(2,128)S(1)} %fusion.41, pred[2432]{0:T(1024)(128)(4,1)S(1)} %broadcast_in_dim.100, f32[2,608,64]{1,2,0:T(8,128)S(1)} %copy-done.2, ...), kind=kOutput, calls=%fused_computation.8.clone.1 | convolution fusion | flops 390598656 | bytes 13086593 | tf_op jit(solution)/shard_map/while/body/eval_jaxpr/hqk,khd->hqd/dot_general | solution.py:40
  120.3 0.7 copy-done.3
  121.2 0.1 broadcast_in_dim.100
  121.3 2.4 %constant_dynamic-slice_fusion.4 = (bf16[1,2432,128]{2,1,0:T(8,128)(2,1)}, bf16[1,2432,128]{2,1,0:T(8,128)(2,1)}) fusion(bf16[2,2432,128]{2,1,0:T(8,128)(2,1)} %get-tuple-element.222, s32[]{:T(128)S(6)} %copy.73, bf16[2,2432,128]{2,1,0:T(8,128)(2,1)} %get-tuple-element.220), kind=kLoop, calls=%fused_computation.16.clone.1 | loop fusion | bytes 2490372 | tf_op jit(solution)/shard_map/while/body/jit(dynamic_index_in_dim)/dynamic_slice | solution.py:70
  123.7 2.1 %copy.66 = bf16[1,2432,128]{1,2,0:T(8,128)(2,1)} copy(bf16[1,2432,128]{2,1,0:T(8,128)(2,1)} %get-tuple-element.189) | data formatting | bytes 1245184 | tf_op jit(solution)/shard_map/while/body/jit(dynamic_index_in_dim)/dynamic_slice | solution.py:70
  125.9 2.1 %copy.67 = bf16[1,2432,128]{1,2,0:T(8,128)(2,1)} copy(bf16[1,2432,128]{2,1,0:T(8,128)(2,1)} %get-tuple-element.193) | data formatting | bytes 1245184 | tf_op jit(solution)/shard_map/while/body/jit(dynamic_index_in_dim)/dynamic_slice | solution.py:70
  128.0 3.1 %bitcast_reduce_fusion.2 = (f32[2,608]{1,0:T(2,128)S(1)}, f32[2,2432,608]{1,2,0:T(8,128)S(1)}) fusion(pred[2432]{0:T(1024)(128)(4,1)S(1)} %broadcast_in_dim.100, bf16[2432,2,64]{0,2,1:T(8,128)(2,1)} %bitcast.60, bf16[608,2,64]{0,2,1:T(8,128)(2,1)S(1)} %get-tuple-element.221), kind=kOutput, calls=%fused_computation.1.clone.1 | convolution fusion | flops 387406656 | bytes 12614784 | tf_op jit(solution)/shard_map/while/body/eval_jaxpr/qhd,khd->hqk/dot_general | solution.py:32
  131.1 2.5 %fusion.42 = f32[2,608]{1,0:T(2,128)S(1)} fusion(f32[2,2432,608]{1,2,0:T(8,128)S(1)} %get-tuple-element.191, f32[2,608]{1,0:T(2,128)S(1)} %fusion.41, pred[2432]{0:T(1024)(128)(4,1)S(1)} %broadcast_in_dim.100), kind=kLoop, calls=%fused_computation.5.clone.1 | loop fusion | flops 11828032 | bytes 11841408 | tf_op jit(solution)/shard_map/while/body/eval_jaxpr/reduce_sum | solution.py:39
  133.7 2.6 %fusion.44 = f32[2,608,64]{1,2,0:T(8,128)S(1)} fusion(bf16[2432,2,64]{0,2,1:T(8,128)(2,1)S(1)} %bitcast.61, f32[2,2432,608]{1,2,0:T(8,128)S(1)} %get-tuple-element.191, f32[2,608]{1,0:T(2,128)S(1)} %fusion.41, pred[2432]{0:T(1024)(128)(4,1)S(1)} %broadcast_in_dim.100, f32[2,608,64]{1,2,0:T(8,128)S(1)} %copy-done.2, ...), kind=kOutput, calls=%fused_computation.8.clone.1 | convolution fusion | flops 390598656 | bytes 13086593 | tf_op jit(solution)/shard_map/while/body/eval_jaxpr/hqk,khd->hqd/dot_general | solution.py:40
  136.4 0.7 copy-done.3
  137.1 1.7 divide_convert_fusion
  138.7 1.1 copy.54
  139.9 0.9 reshape.128
  140.7 4.6 %all-to-all-start.1 = ((bf16[4,2,9728]{2,1,0:T(2,128)(2,1)}), bf16[4,2,9728]{2,1,0:T(2,128)(2,1)}, u32[]{:S(2)}, u32[]{:S(2)}) async-start(bf16[4,2,9728]{2,1,0:T(2,128)(2,1)} %reshape.128), calls=%async_computation.1 | async-start | bytes 311296 | tf_op jit(solution)/shard_map/all_to_all | solution.py:115
  145.4 0.1 broadcast_in_dim.59
  145.5 6.6 %all-to-all-done.1 = bf16[4,2,9728]{2,1,0:T(2,128)(2,1)} async-done(((bf16[4,2,9728]{2,1,0:T(2,128)(2,1)}), bf16[4,2,9728]{2,1,0:T(2,128)(2,1)}, u32[]{:S(2)}, u32[]{:S(2)}) %all-to-all-start.1) | async-done | bytes 155680 | tf_op jit(solution)/shard_map/all_to_all | solution.py:115
  152.1 1.2 reshape.129
  153.3 0.9 copy.63
  154.2 1.2 reshape.118
  155.4 2.5 %fusion.15 = bf16[152,1024]{1,0:T(8,128)(2,1)} fusion(f32[152,1024]{1,0:T(8,128)} %reshape.120, bf16[152,512]{1,0:T(8,128)(2,1)S(1)} %reshape.118, bf16[512,1024]{1,0:T(8,128)(2,1)} %param.13, pred[152]{0:T(512)(128)(4,1)S(1)} %broadcast_in_dim.59), kind=kOutput, calls=%fused_computation.25 | convolution fusion | flops 159850496 | bytes 2138264 | tf_op jit(solution)/shard_map/dot_general | solution.py:117
  157.9 1.1 reshape.119
  158.9 1.0 copy.56
  (42 shorter events, 0.9 us)
Async XLA Ops:
  6.5 6.9 %copy-start = (bf16[1024,1536]{1,0:T(8,128)(2,1)S(1)}, bf16[1024,1536]{1,0:T(8,128)(2,1)}, u32[]{:S(2)}) copy-start(bf16[1024,1536]{1,0:T(8,128)(2,1)} %param.12) | copy-start | bytes 9437188
  6.5 50.4 %copy-start.4 = (u32[32]{0:T(128)S(1)}, u32[32]{0:T(128)}, u32[]{:S(2)}) copy-start(u32[32]{0:T(128)} %constant.36) | copy-start | bytes 388
  6.5 72.3 %all-gather.5.cloned.1.call-start = ((), (), s32[]{:S(2)}) async-start(), calls=%async_computation.3 | async-start | bytes 1400832 | tf_op jit(solution)/shard_map/all_gather | solution.py:107
  55.4 49.6 %all-gather.3.cloned.1.call-start = ((), (), s32[]{:S(2)}) async-start(), calls=%async_computation.2 | async-start | bytes 1400832 | tf_op jit(solution)/shard_map/all_gather | solution.py:106
  111.9 5.7 %copy-start.1 = (bf16[1,2432,128]{1,2,0:T(8,128)(2,1)S(1)}, bf16[1,2432,128]{1,2,0:T(8,128)(2,1)}, u32[]{:S(2)}) copy-start(bf16[1,2432,128]{1,2,0:T(8,128)(2,1)} %copy.67) | copy-start | bytes 1867780 | tf_op jit(solution)/shard_map/while
  111.9 5.7 %copy-start.2 = (f32[2,608,64]{1,2,0:T(8,128)S(1)}, f32[2,608,64]{1,2,0:T(8,128)}, u32[]{:S(2)}) copy-start(f32[2,608,64]{1,2,0:T(8,128)} %get-tuple-element.208) | copy-start | bytes 933892 | tf_op jit(solution)/shard_map/while
  120.3 0.7 copy-start.3
  128.0 5.7 %copy-start.1 = (bf16[1,2432,128]{1,2,0:T(8,128)(2,1)S(1)}, bf16[1,2432,128]{1,2,0:T(8,128)(2,1)}, u32[]{:S(2)}) copy-start(bf16[1,2432,128]{1,2,0:T(8,128)(2,1)} %copy.67) | copy-start | bytes 1867780 | tf_op jit(solution)/shard_map/while
  128.0 5.7 %copy-start.2 = (f32[2,608,64]{1,2,0:T(8,128)S(1)}, f32[2,608,64]{1,2,0:T(8,128)}, u32[]{:S(2)}) copy-start(f32[2,608,64]{1,2,0:T(8,128)} %get-tuple-element.208) | copy-start | bytes 933892 | tf_op jit(solution)/shard_map/while
  136.3 0.7 copy-start.3
  140.7 11.3 %all-to-all-start.1 = ((bf16[4,2,9728]{2,1,0:T(2,128)(2,1)}), bf16[4,2,9728]{2,1,0:T(2,128)(2,1)}, u32[]{:S(2)}, u32[]{:S(2)}) async-start(bf16[4,2,9728]{2,1,0:T(2,128)(2,1)} %reshape.128), calls=%async_computation.1 | async-start | bytes 311296 | tf_op jit(solution)/shard_map/all_to_all | solution.py:115
Sparse Core Ops, SparseCore 0:
  55.5 23.2 all-gather.4
  80.7 24.1 all-gather.2
where the time goes:
time: 168 us; the launch traced here: 167 us
  waiting for transfers between devices  45.1 us (27%)
  local copies, waits for them, and re-layouts  41.4 us (25%)
  blocking collectives  34.5 us (21%)
  matrix products  16.6 us (10%)
  between operations  14.8 us (9%)
  other arithmetic  9.53 us (6%)
  starting transfers between devices  4.64 us (3%)
    all_to_all x1, blocking collectives, on_device(): lax.all_to_all(stacked, 'frame', split_axis=2, concat_axis=0, tiled=True)  26.5 us
    all_gather x1, waiting for transfers between devices, on_device(): lax.all_gather(key_local, 'space', axis=0, tiled=True)  26.1 us
    dynamic_slice x6, local copies, waits for them, and re-layouts, fold_masked(): lax.scan(step_group, carry, (key_groups, value_groups, count_groups))  13.3 us
    all_gather x1, waiting for transfers between devices, on_device(): lax.all_gather(value_local, 'space', axis=0, tiled=True)  12.4 us
    unnamed x1, blocking collectives  8.09 us
    all_to_all x1, waiting for transfers between devices, on_device(): lax.all_to_all(attended, 'frame', split_axis=0, concat_axis=1, tiled=True)  6.57 us
    dot_general x2, matrix products, attend(): jnp.einsum('qhd,khd->hqk', query_heads, key_heads, preferred_element_type...  6.27 us
    dot_general x2, matrix products, attend(): jnp.einsum('hqk,khd->hqd', weights.astype(jnp.bfloat16), value_heads, pre...  5.28 us
  transfers between devices with their start and end apart: 3, of which 3 were waited for; matrix products, arithmetic and copies ran while one was open for 1% of the time, Pallas kernels for 0%

commit v1 on v0

--- a/solution.py
+++ b/solution.py
@@ -93,7 +93,9 @@
     frames = lax.axis_size("frame")
     local_heads = HEADS // frames
     stacked = projected.reshape(rows_dev, 3, HEADS, head_size)
-    regrouped = lax.all_to_all(stacked, "frame", split_axis=2, concat_axis=0, tiled=True)
+    parts = jnp.split(stacked, lax.axis_size("frame"), axis=2)
+    received = lax.all_to_all(jnp.stack(parts), "frame", 0, 0)
+    regrouped = jnp.concatenate(received, axis=0)
     all_rows = regrouped.shape[0]
     query_local = regrouped[:, 0]
     key_local = regrouped[:, 1].reshape(all_rows, local_heads * head_size)

time: 168 us -> 174 us (1.036)
  local copies, waits for them, and re-layouts: 41.4 us -> 45 us
  other arithmetic: 9.53 us -> 12.3 us
    another operation x0 -> x2, local copies, waits for them, and re-layouts: none -> 6.34 us  [on_device(): received = lax.all_to_all(jnp.stack(parts), 'frame', 0, 0)]
    reshape x2 -> x1, local copies, waits for them, and re-layouts: 5.19 us -> 2.39 us  [on_device(): stacked = projected.reshape(rows_dev, 3, HEADS, head_size)]
    another operation x0 -> x1, other arithmetic: none -> 2.72 us  [on_device(): received = lax.all_to_all(jnp.stack(parts), 'frame', 0, 0)]
    all_to_all x2 -> x1, local copies, waits for them, and re-layouts: 4.17 us -> 1.5 us  [on_device(): received = lax.all_to_all(jnp.stack(parts), 'frame', 0, 0)]
    reshape x0 -> x1, local copies, waits for them, and re-layouts: none -> 2.67 us  [on_device(): regrouped = jnp.concatenate(received, axis=0)]
where the time goes in v1:
time: 174 us; the launch traced here: 173 us
  waiting for transfers between devices  45.1 us (26%)
  local copies, waits for them, and re-layouts  45 us (26%)
  blocking collectives  34.5 us (20%)
  matrix products  16.6 us (10%)
  between operations  14.8 us (9%)
  other arithmetic  12.3 us (7%)
  starting transfers between devices  4.64 us (3%)
    all_to_all x1, blocking collectives, on_device(): received = lax.all_to_all(jnp.stack(parts), 'frame', 0, 0)  26.5 us
    all_gather x1, waiting for transfers between devices, on_device(): lax.all_gather(key_local, 'space', axis=0, tiled=True)  26.1 us
    dynamic_slice x6, local copies, waits for them, and re-layouts, fold_masked(): lax.scan(step_group, carry, (key_groups, value_groups, count_groups))  13.4 us
    all_gather x1, waiting for transfers between devices, on_device(): lax.all_gather(value_local, 'space', axis=0, tiled=True)  12.4 us
    unnamed x1, blocking collectives  8.08 us
    all_to_all x1, waiting for transfers between devices, on_device(): lax.all_to_all(attended, 'frame', split_axis=0, concat_axis=1, tiled=True)  6.57 us
    another operation x2, local copies, waits for them, and re-layouts, on_device(): received = lax.all_to_all(jnp.stack(parts), 'frame', 0, 0)  6.34 us
    dot_general x2, matrix products, attend(): jnp.einsum('qhd,khd->hqk', query_heads, key_heads, preferred_element_type...  6.26 us
  transfers between devices with their start and end apart: 3, of which 3 were waited for; matrix products, arithmetic and copies ran while one was open for 1% of the time, Pallas kernels for 0%

profile of v1, /device:TPU:0, one launch (start us, length us, event | category | flops | bytes accessed | tf_op | source)
XLA Modules:
  0.0 173.1 jit_solution(9026521304486175056)
XLA Ops:
  6.5 1.3 convert_reduce_fusion
  8.0 1.3 multiply_reduce_fusion
  9.3 1.9 %copy.55 = f32[4,38,1024]{2,1,0:T(8,128)} copy(bf16[4,38,1024]{2,0,1:T(4,128)(2,1)} %param.8) | data formatting | bytes 933888 | tf_op jit(solution)/shard_map/convert_element_type | solution.py:119
  11.4 2.0 %reshape.124 = f32[152,1024]{1,0:T(8,128)} reshape(f32[4,38,1024]{2,1,0:T(8,128)} %copy.55) | data formatting | bytes 1245184 | tf_op jit(solution)/shard_map/convert_element_type | solution.py:119
  13.4 2.6 %convolution_convert_fusion = bf16[152,1536]{1,0:T(8,128)(2,1)} fusion(bf16[1024,1536]{1,0:T(8,128)(2,1)S(1)} %copy-done, f32[152,1024]{1,0:T(8,128)} %reshape.124, f32[1024]{0:T(1024)} %param.11, f32[1024]{0:T(1024)} %param.10, f32[152]{0:T(256)S(1)} %rsqrt.12, f32[152]{0:T(256)S(1)} %div.17), kind=kOutput, calls=%fused_computation.22 | convolution fusion | flops 479162368 | bytes 4244672 | tf_op jit(solution)/shard_map/dot_general | solution.py:91
  16.1 2.4 %reshape.118 = bf16[152,3,8,64]{3,2,1,0:T(8,128)(2,1)} reshape(bf16[152,1536]{1,0:T(8,128)(2,1)} %convolution_convert_fusion) | data formatting | bytes 933888 | tf_op jit(solution)/shard_map/reshape | solution.py:95
  18.5 3.2 %slice_bitcast_fusion.3 = (bf16[1,152,3,2,64]{4,3,2,1,0:T(2,128)(2,1)S(1)}, bf16[1,152,3,2,64]{4,3,2,1,0:T(2,128)(2,1)S(1)}, bf16[1,152,3,2,64]{4,3,2,1,0:T(2,128)(2,1)S(1)}, bf16[1,152,3,2,64]{4,3,2,1,0:T(2,128)(2,1)S(1)}) fusion(bf16[152,3,8,64]{3,2,1,0:T(8,128)(2,1)} %reshape.118), kind=kLoop, calls=%fused_computation.39 | loop fusion | bytes 933888 | tf_op jit(solution)/shard_map/stack | solution.py:97
  21.7 2.7 %pad_maximum_fusion = bf16[4,152,3,2,64]{4,3,2,1,0:T(2,128)(2,1)} fusion(bf16[1,152,3,2,64]{4,3,2,1,0:T(2,128)(2,1)S(1)} %get-tuple-element.140, bf16[1,152,3,2,64]{4,3,2,1,0:T(2,128)(2,1)S(1)} %get-tuple-element.141, bf16[1,152,3,2,64]{4,3,2,1,0:T(2,128)(2,1)S(1)} %get-tuple-element.142, bf16[1,152,3,2,64]{4,3,2,1,0:T(2,128)(2,1)S(1)} %get-tuple-element.139), kind=kLoop, calls=%fused_computation.26 | loop fusion | flops 700416 | bytes 933888 | tf_op jit(solution)/shard_map/stack | solution.py:97
  24.4 3.1 %copy.59 = bf16[4,152,3,2,64]{1,4,3,2,0:T(8,128)(2,1)} copy(bf16[4,152,3,2,64]{4,3,2,1,0:T(2,128)(2,1)} %pad_maximum_fusion) | data formatting | bytes 933888 | tf_op jit(solution)/shard_map/stack | solution.py:97
  27.5 26.5 %all_to_all.20 = bf16[4,152,3,2,64]{1,4,3,2,0:T(8,128)(2,1)S(1)} all-to-all(bf16[4,152,3,2,64]{1,4,3,2,0:T(8,128)(2,1)} %copy.59), channel_id=1, replica_groups=mesh['frame'=4,'space'=8] {'frame'}, dimensions={0} | all-to-all | bytes 933888 | tf_op jit(solution)/shard_map/all_to_all | solution.py:97
  54.0 1.5 copy.60
  55.5 2.7 %reshape.119 = bf16[608,3,2,64]{0,3,2,1:T(8,128)(2,1)} reshape(bf16[4,152,3,2,64]{1,0,4,3,2:T(4,128)(2,1)} %copy.60) | data formatting | bytes 933888 | tf_op jit(solution)/shard_map/reshape | solution.py:98
  58.2 1.8 %fusion.20 = (bf16[608,1,2,64]{0,3,2,1:T(8,128)(2,1)}, bf16[608,2,64]{0,2,1:T(8,128)(2,1)S(1)}, bf16[608,1,2,64]{0,3,2,1:T(8,128)(2,1)S(1)}) fusion(bf16[608,3,2,64]{0,3,2,1:T(8,128)(2,1)} %reshape.119), kind=kLoop, calls=%fused_computation.45 | loop fusion | bytes 933888 | tf_op jit(solution)/shard_map/slice | solution.py:102
  59.9 1.7 copy.62
  61.7 0.8 copy.61
  63.2 0.6 dynamic-slice
  64.5 8.1 %all-reduce = s32[32]{0:T(128)S(1)} all-reduce(s32[32]{0:T(128)S(1)} %broadcast_dynamic-update-slice_fusion), channel_id=1, replica_groups=mesh['frame'=4,'space'=8] {'space'}, use_global_device_ids=true, to_apply=%add | all-reduce | flops 32 | bytes 256
  72.7 12.4 %all-gather.5.cloned.1.call-done = bf16[4864,128]{1,0:T(8,128)(2,1)} async-done(((bf16[608,128]{1,0:T(8,128)(2,1)}), bf16[4864,128]{1,0:T(8,128)(2,1)}) %all-gather.5.cloned.1.call-update) | async-done | bytes 1245200 | tf_op jit(solution)/shard_map/all_gather | solution.py:109
  85.1 26.1 %all-gather.3.cloned.1.call-done = bf16[4864,128]{1,0:T(8,128)(2,1)} async-done(((bf16[608,128]{1,0:T(8,128)(2,1)}), bf16[4864,128]{1,0:T(8,128)(2,1)}) %all-gather.3.cloned.1.call-update) | async-done | bytes 1245200 | tf_op jit(solution)/shard_map/all_gather | solution.py:108
  111.2 32.2 %while.15 = (s32[]{:T(128)}, f32[2,608]{1,0:T(2,128)S(1)}, f32[2,608]{1,0:T(2,128)S(1)}, f32[2,608,64]{1,2,0:T(8,128)}, s32[2,16]{1,0:T(2,128)S(1)}, /*index=5*/...) while((s32[]{:T(128)}, f32[2,608]{1,0:T(2,128)S(1)}, ...), condition=%wide.region_5.6_spmd.clone, body=%wide.region_2.5_spmd.clone.sunk | while | flops 789841920 | bytes 47565588 | solution.py:70
  111.4 0.1 broadcast_in_dim.100
  111.6 2.4 %constant_dynamic-slice_fusion.4 = (bf16[1,2432,128]{2,1,0:T(8,128)(2,1)}, bf16[1,2432,128]{2,1,0:T(8,128)(2,1)}) fusion(bf16[2,2432,128]{2,1,0:T(8,128)(2,1)} %get-tuple-element.234, s32[]{:T(128)S(6)} %copy.86, bf16[2,2432,128]{2,1,0:T(8,128)(2,1)} %get-tuple-element.232), kind=kLoop, calls=%fused_computation.16.clone.1 | loop fusion | bytes 2490372 | tf_op jit(solution)/shard_map/while/body/jit(dynamic_index_in_dim)/dynamic_slice | solution.py:70
  114.0 2.1 %copy.79 = bf16[1,2432,128]{1,2,0:T(8,128)(2,1)} copy(bf16[1,2432,128]{2,1,0:T(8,128)(2,1)} %get-tuple-element.201) | data formatting | bytes 1245184 | tf_op jit(solution)/shard_map/while/body/jit(dynamic_index_in_dim)/dynamic_slice | solution.py:70
  116.1 2.2 %copy.80 = bf16[1,2432,128]{1,2,0:T(8,128)(2,1)} copy(bf16[1,2432,128]{2,1,0:T(8,128)(2,1)} %get-tuple-element.205) | data formatting | bytes 1245184 | tf_op jit(solution)/shard_map/while/body/jit(dynamic_index_in_dim)/dynamic_slice | solution.py:70
  118.2 3.1 %bitcast_reduce_fusion.2 = (f32[2,608]{1,0:T(2,128)S(1)}, f32[2,2432,608]{1,2,0:T(8,128)S(1)}) fusion(pred[2432]{0:T(1024)(128)(4,1)S(1)} %broadcast_in_dim.100, bf16[2432,2,64]{0,2,1:T(8,128)(2,1)} %bitcast.65, bf16[608,2,64]{0,2,1:T(8,128)(2,1)S(1)} %get-tuple-element.233), kind=kOutput, calls=%fused_computation.1.clone.1 | convolution fusion | flops 387406656 | bytes 12614784 | tf_op jit(solution)/shard_map/while/body/eval_jaxpr/qhd,khd->hqk/dot_general | solution.py:32
  121.4 2.5 %fusion.42 = f32[2,608]{1,0:T(2,128)S(1)} fusion(f32[2,2432,608]{1,2,0:T(8,128)S(1)} %get-tuple-element.203, f32[2,608]{1,0:T(2,128)S(1)} %fusion.41, pred[2432]{0:T(1024)(128)(4,1)S(1)} %broadcast_in_dim.100), kind=kLoop, calls=%fused_computation.5.clone.1 | loop fusion | flops 11828032 | bytes 11841408 | tf_op jit(solution)/shard_map/while/body/eval_jaxpr/reduce_sum | solution.py:39
  123.9 2.6 %fusion.44 = f32[2,608,64]{1,2,0:T(8,128)S(1)} fusion(bf16[2432,2,64]{0,2,1:T(8,128)(2,1)S(1)} %bitcast.66, f32[2,2432,608]{1,2,0:T(8,128)S(1)} %get-tuple-element.203, f32[2,608]{1,0:T(2,128)S(1)} %fusion.41, pred[2432]{0:T(1024)(128)(4,1)S(1)} %broadcast_in_dim.100, f32[2,608,64]{1,2,0:T(8,128)S(1)} %copy-done.2, ...), kind=kOutput, calls=%fused_computation.8.clone.1 | convolution fusion | flops 390598656 | bytes 13086593 | tf_op jit(solution)/shard_map/while/body/eval_jaxpr/hqk,khd->hqd/dot_general | solution.py:40
  126.6 0.7 copy-done.3
  127.5 0.1 broadcast_in_dim.100
  127.7 2.4 %constant_dynamic-slice_fusion.4 = (bf16[1,2432,128]{2,1,0:T(8,128)(2,1)}, bf16[1,2432,128]{2,1,0:T(8,128)(2,1)}) fusion(bf16[2,2432,128]{2,1,0:T(8,128)(2,1)} %get-tuple-element.234, s32[]{:T(128)S(6)} %copy.86, bf16[2,2432,128]{2,1,0:T(8,128)(2,1)} %get-tuple-element.232), kind=kLoop, calls=%fused_computation.16.clone.1 | loop fusion | bytes 2490372 | tf_op jit(solution)/shard_map/while/body/jit(dynamic_index_in_dim)/dynamic_slice | solution.py:70
  130.0 2.1 %copy.79 = bf16[1,2432,128]{1,2,0:T(8,128)(2,1)} copy(bf16[1,2432,128]{2,1,0:T(8,128)(2,1)} %get-tuple-element.201) | data formatting | bytes 1245184 | tf_op jit(solution)/shard_map/while/body/jit(dynamic_index_in_dim)/dynamic_slice | solution.py:70
  132.2 2.2 %copy.80 = bf16[1,2432,128]{1,2,0:T(8,128)(2,1)} copy(bf16[1,2432,128]{2,1,0:T(8,128)(2,1)} %get-tuple-element.205) | data formatting | bytes 1245184 | tf_op jit(solution)/shard_map/while/body/jit(dynamic_index_in_dim)/dynamic_slice | solution.py:70
  134.3 3.1 %bitcast_reduce_fusion.2 = (f32[2,608]{1,0:T(2,128)S(1)}, f32[2,2432,608]{1,2,0:T(8,128)S(1)}) fusion(pred[2432]{0:T(1024)(128)(4,1)S(1)} %broadcast_in_dim.100, bf16[2432,2,64]{0,2,1:T(8,128)(2,1)} %bitcast.65, bf16[608,2,64]{0,2,1:T(8,128)(2,1)S(1)} %get-tuple-element.233), kind=kOutput, calls=%fused_computation.1.clone.1 | convolution fusion | flops 387406656 | bytes 12614784 | tf_op jit(solution)/shard_map/while/body/eval_jaxpr/qhd,khd->hqk/dot_general | solution.py:32
  137.5 2.5 %fusion.42 = f32[2,608]{1,0:T(2,128)S(1)} fusion(f32[2,2432,608]{1,2,0:T(8,128)S(1)} %get-tuple-element.203, f32[2,608]{1,0:T(2,128)S(1)} %fusion.41, pred[2432]{0:T(1024)(128)(4,1)S(1)} %broadcast_in_dim.100), kind=kLoop, calls=%fused_computation.5.clone.1 | loop fusion | flops 11828032 | bytes 11841408 | tf_op jit(solution)/shard_map/while/body/eval_jaxpr/reduce_sum | solution.py:39
  140.0 2.6 %fusion.44 = f32[2,608,64]{1,2,0:T(8,128)S(1)} fusion(bf16[2432,2,64]{0,2,1:T(8,128)(2,1)S(1)} %bitcast.66, f32[2,2432,608]{1,2,0:T(8,128)S(1)} %get-tuple-element.203, f32[2,608]{1,0:T(2,128)S(1)} %fusion.41, pred[2432]{0:T(1024)(128)(4,1)S(1)} %broadcast_in_dim.100, f32[2,608,64]{1,2,0:T(8,128)S(1)} %copy-done.2, ...), kind=kOutput, calls=%fused_computation.8.clone.1 | convolution fusion | flops 390598656 | bytes 13086593 | tf_op jit(solution)/shard_map/while/body/eval_jaxpr/hqk,khd->hqd/dot_general | solution.py:40
  142.7 0.7 copy-done.3
  143.4 1.7 divide_convert_fusion
  145.1 1.1 copy.67
  146.2 0.9 reshape.132
  147.1 4.6 %all-to-all-start.1 = ((bf16[4,2,9728]{2,1,0:T(2,128)(2,1)}), bf16[4,2,9728]{2,1,0:T(2,128)(2,1)}, u32[]{:S(2)}, u32[]{:S(2)}) async-start(bf16[4,2,9728]{2,1,0:T(2,128)(2,1)} %reshape.132), calls=%async_computation.1 | async-start | bytes 311296 | tf_op jit(solution)/shard_map/all_to_all | solution.py:117
  151.8 0.1 broadcast_in_dim.59
  151.8 6.6 %all-to-all-done.1 = bf16[4,2,9728]{2,1,0:T(2,128)(2,1)} async-done(((bf16[4,2,9728]{2,1,0:T(2,128)(2,1)}), bf16[4,2,9728]{2,1,0:T(2,128)(2,1)}, u32[]{:S(2)}, u32[]{:S(2)}) %all-to-all-start.1) | async-done | bytes 155680 | tf_op jit(solution)/shard_map/all_to_all | solution.py:117
  158.4 1.2 reshape.133
  159.6 0.9 copy.76
  160.5 1.2 reshape.122
  161.7 2.5 %fusion.15 = bf16[152,1024]{1,0:T(8,128)(2,1)} fusion(f32[152,1024]{1,0:T(8,128)} %reshape.124, bf16[152,512]{1,0:T(8,128)(2,1)S(1)} %reshape.122, bf16[512,1024]{1,0:T(8,128)(2,1)} %param.13, pred[152]{0:T(512)(128)(4,1)S(1)} %broadcast_in_dim.59), kind=kOutput, calls=%fused_computation.25 | convolution fusion | flops 159850496 | bytes 2138264 | tf_op jit(solution)/shard_map/dot_general | solution.py:119
  164.2 1.1 reshape.123
  165.3 1.0 copy.69
  (44 shorter events, 1.1 us)
Async XLA Ops:
  6.5 6.9 %copy-start = (bf16[1024,1536]{1,0:T(8,128)(2,1)S(1)}, bf16[1024,1536]{1,0:T(8,128)(2,1)}, u32[]{:S(2)}) copy-start(bf16[1024,1536]{1,0:T(8,128)(2,1)} %param.12) | copy-start | bytes 9437188
  6.5 56.7 %copy-start.4 = (u32[32]{0:T(128)S(1)}, u32[32]{0:T(128)}, u32[]{:S(2)}) copy-start(u32[32]{0:T(128)} %constant.36) | copy-start | bytes 388
  6.5 78.6 %all-gather.5.cloned.1.call-start = ((), (), s32[]{:S(2)}) async-start(), calls=%async_computation.3 | async-start | bytes 1400832 | tf_op jit(solution)/shard_map/all_gather | solution.py:109
  61.7 49.6 %all-gather.3.cloned.1.call-start = ((), (), s32[]{:S(2)}) async-start(), calls=%async_computation.2 | async-start | bytes 1400832 | tf_op jit(solution)/shard_map/all_gather | solution.py:108
  118.2 5.7 %copy-start.1 = (bf16[1,2432,128]{1,2,0:T(8,128)(2,1)S(1)}, bf16[1,2432,128]{1,2,0:T(8,128)(2,1)}, u32[]{:S(2)}) copy-start(bf16[1,2432,128]{1,2,0:T(8,128)(2,1)} %copy.80) | copy-start | bytes 1867780 | tf_op jit(solution)/shard_map/while
  118.2 5.7 %copy-start.2 = (f32[2,608,64]{1,2,0:T(8,128)S(1)}, f32[2,608,64]{1,2,0:T(8,128)}, u32[]{:S(2)}) copy-start(f32[2,608,64]{1,2,0:T(8,128)} %get-tuple-element.220) | copy-start | bytes 933892 | tf_op jit(solution)/shard_map/while
  126.6 0.7 copy-start.3
  134.3 5.7 %copy-start.1 = (bf16[1,2432,128]{1,2,0:T(8,128)(2,1)S(1)}, bf16[1,2432,128]{1,2,0:T(8,128)(2,1)}, u32[]{:S(2)}) copy-start(bf16[1,2432,128]{1,2,0:T(8,128)(2,1)} %copy.80) | copy-start | bytes 1867780 | tf_op jit(solution)/shard_map/while
  134.3 5.7 %copy-start.2 = (f32[2,608,64]{1,2,0:T(8,128)S(1)}, f32[2,608,64]{1,2,0:T(8,128)}, u32[]{:S(2)}) copy-start(f32[2,608,64]{1,2,0:T(8,128)} %get-tuple-element.220) | copy-start | bytes 933892 | tf_op jit(solution)/shard_map/while
  142.7 0.7 copy-start.3
  147.1 11.3 %all-to-all-start.1 = ((bf16[4,2,9728]{2,1,0:T(2,128)(2,1)}), bf16[4,2,9728]{2,1,0:T(2,128)(2,1)}, u32[]{:S(2)}, u32[]{:S(2)}) async-start(bf16[4,2,9728]{2,1,0:T(2,128)(2,1)} %reshape.132), calls=%async_computation.1 | async-start | bytes 311296 | tf_op jit(solution)/shard_map/all_to_all | solution.py:117
Sparse Core Ops, SparseCore 0:
  61.8 23.2 all-gather.4
  87.0 24.1 all-gather.2
